TPU v7x, 32 devices: a whole 2x2x4 slice. The times are simulated.
32 devices in a mesh: row: 8 (over z, y), col: 4 (over x, core).
Axes of the slice: x: 2, y: 2, z: 4, core: 2. Of those that a mesh axis runs over, the one named last changes fastest.
Arguments:
- matrix_tiles: float32 [8, 4, 16, 256, 256], P('row', 'col'), may hold values from -0.3125 to 0.3125
- tile_slot: int32 [8, 4, 16], P('row', 'col'), may hold values from 0 to 2047, as said below
- cost_vector: float32 [512, 256], P('col'), may hold values from -24 to 24
- lower_bound: float32 [512, 256], P('col'), may hold values from -4 to 4
- bound_width: float32 [512, 256], P('col'), may hold values from 0.5 to 4
- variable_kind: int32 [512, 256], P('col'), may hold values from 0 to 2
- right_side: float32 [128, 256], P('row'), may hold values from -24 to 24
- row_kind: int32 [128, 256], P('row'), may hold values from 0 to 1
- primal_start: float32 [512, 256], P('col'), may hold values from -6 to 6
- dual_start: float32 [128, 256], P('row'), may hold values from -3 to 3
- primal_weight: float32 [], replicated, may hold values from 0.7 to 1.4
- step_start: float32 [], replicated, may hold values from 1 to 2
Outputs:
- primal: float32 [512, 256], P('col')
- dual: float32 [128, 256], P('row')
Inputs may be any that keep to these rules, and one draw needn't show every extreme that they name: `tile_slot`: within each block [r, c] the 16 tiles lie in different column tiles. Split a block's 128 column tiles into runs of 16 in a row: no run holds more than 2 of the block's tiles.
All inputs are finite; a program needn't handle non-finite values.
Results may differ from a plain program's by a relative error of at most 0.00026.
Values sent between devices are 32-bit elements; how exact they have to be, the bound alone decides.
No kernel may reach another device: no remote copies, remote signals or barrier semaphores. Data moves between devices by JAX's collectives and lax.ppermute only.
A program may use at most 64 MiB of HBM per device.

v0:
```python
import jax
import jax.numpy as jnp
from jax import lax
from jax.sharding import PartitionSpec as P

ITERS = 4
highest = lax.Precision.HIGHEST


def project_primal(values, lower_bound, bound_width, variable_kind):
    lifted = jnp.where(variable_kind >= 1, jnp.maximum(values, lower_bound), values)
    return jnp.where(variable_kind == 2, jnp.minimum(lifted, lower_bound + bound_width), lifted)


def project_dual(values, row_kind):
    return jnp.where(row_kind == 1, jnp.maximum(values, 0.0), values)


def next_step(cross, dual_square, primal_square, weight, step_size, iteration):
    movement = 0.5 * weight * primal_square + 0.5 * dual_square / weight
    count = iteration + 11.0
    return movement / jnp.maximum(
        jnp.abs(cross) / (1.0 - count ** (-0.3)), movement / ((1.0 + count ** (-0.6)) * step_size)
    )


def shards(
    matrix_tiles,
    tile_slot,
    cost_vector,
    lower_bound,
    bound_width,
    variable_kind,
    right_side,
    row_kind,
    primal_start,
    dual_start,
    primal_weight,
    step_start,
):
    tile_set = matrix_tiles[0, 0]
    slots = tile_slot[0, 0]
    row_tiles, tile_width = right_side.shape
    col_tiles = cost_vector.shape[0]
    tile_count = slots.shape[0]
    row_count = lax.axis_size("row")
    row_of = slots // col_tiles
    col_of = slots % col_tiles
    row_onehot = (row_of[None, :] == jnp.arange(row_tiles, dtype=jnp.int32)[:, None]).astype(
        jnp.float32
    )

    def forward_picked(picked):
        product = jnp.einsum("tij,tj->ti", tile_set, picked, precision=highest)
        partial_rows = jnp.dot(row_onehot, product, precision=highest)
        return lax.psum(partial_rows, "col")

    def backward_product(vector):
        picked = vector[row_of]
        return jnp.einsum("tij,ti->tj", tile_set, picked, precision=highest)

    share_len = col_tiles * tile_width // row_count
    offset = lax.axis_index("row") * share_len

    def take_share(values):
        return lax.dynamic_slice_in_dim(values.reshape(-1), offset, share_len, 0)

    share_tiles = col_tiles // row_count
    capacity = (tile_count + row_count - 1) // row_count
    share_of = col_of // share_tiles
    counter = jnp.arange(tile_count, dtype=jnp.int32)
    earlier = (counter[None, :] < counter[:, None]) & (share_of[None, :] == share_of[:, None])
    position = jnp.sum(earlier.astype(jnp.int32), axis=1)
    destination = share_of * capacity + position
    send_hit = destination[None, :] == jnp.arange(row_count * capacity, dtype=jnp.int32)[:, None]
    send_onehot = send_hit.astype(jnp.float32)
    local_index = col_of % share_tiles
    occupied = jnp.sum(send_hit.astype(jnp.int32), axis=1)
    send_index = jnp.where(
        occupied > 0, jnp.sum(jnp.where(send_hit, local_index[None, :], 0), axis=1), -1
    )
    recv_index = lax.all_to_all(send_index, "row", split_axis=0, concat_axis=0, tiled=True)
    recv_onehot = (recv_index[None, :] == jnp.arange(share_tiles, dtype=jnp.int32)[:, None]).astype(
        jnp.float32
    )
    cost_share = take_share(cost_vector)
    lower_share = take_share(lower_bound)
    width_share = take_share(bound_width)
    kind_share = take_share(variable_kind)

    def reduce_back(vector):
        sent = jnp.dot(send_onehot, backward_product(vector), precision=highest)
        arrived = lax.all_to_all(sent, "row", split_axis=0, concat_axis=0, tiled=True)
        return jnp.dot(recv_onehot, arrived, precision=highest).reshape(-1)

    primal = take_share(primal_start)
    image = forward_picked(primal_start[col_of])
    dual = dual_start
    step_size = step_start
    gradient = reduce_back(dual)
    for iteration in range(ITERS):
        primal_next = project_primal(
            primal - step_size / primal_weight * (cost_share - gradient),
            lower_share,
            width_share,
            kind_share,
        )
        back = jnp.dot(
            recv_onehot.T, primal_next.reshape(share_tiles, tile_width), precision=highest
        )
        returned = lax.all_to_all(back, "row", split_axis=0, concat_axis=0, tiled=True)
        image_next = forward_picked(jnp.dot(send_onehot.T, returned, precision=highest))
        dual_next = project_dual(
            dual + step_size * primal_weight * (right_side - 2.0 * image_next + image), row_kind
        )
        if iteration + 1 < ITERS:
            gradient = reduce_back(dual_next)
            change_dual = dual_next - dual
            change_primal = primal_next - primal
            cross_part = jnp.sum(change_dual * (image_next - image))
            dual_part = jnp.sum(change_dual * change_dual)
            primal_part = jnp.sum(change_primal * change_primal)
            cross, dual_square, primal_rows = lax.psum((cross_part, dual_part, primal_part), "row")
            primal_square = lax.psum(primal_rows, "col")
            step_size = next_step(
                cross, dual_square, primal_square, primal_weight, step_size, iteration
            )
        primal, dual, image = (primal_next, dual_next, image_next)
    primal = lax.all_gather(primal, "row", axis=0, tiled=True).reshape(col_tiles, tile_width)
    return (primal, dual)


def solution(mesh):
    return jax.shard_map(
        shards,
        mesh=mesh,
        in_specs=(
            P("row", "col", None, None, None),
            P("row", "col", None),
            P("col", None),
            P("col", None),
            P("col", None),
            P("col", None),
            P("row", None),
            P("row", None),
            P("col", None),
            P("row", None),
            P(),
            P(),
        ),
        out_specs=(P("col", None), P("row", None)),
        check_vma=False,
    )
```

profile of v0, /device:TPU:0, one launch (start us, length us, event | category | flops | bytes accessed | tf_op | source)
XLA Modules:
  0.0 292.4 jit_solution(2359915443829012869)
XLA Ops:
  2.4 7.3 %all-to-all-start = ((s32[8,2,1]{1,2,0:T(1,128)}), s32[8,2,1]{1,2,0:T(1,128)S(1)}, u32[]{:S(2)}, u32[]{:S(2)}) async-start(s32[8,2,1]{1,2,0:T(1,128)} %bitcast.1), calls=%async_computation | async-start | bytes 8192 | tf_op jit(solution)/shard_map/all_to_all | solution.py:82
  11.7 4.3 %fusion.16 = f32[16,1,256]{2,1,0:T(1,128)S(1)} fusion(f32[1,1,16,256,256]{4,3,2,1,0:T(8,128)} %param.12, f32[16,256,1]{1,0,2:T(8,128)S(1)} %bitcast.156), kind=kOutput, calls=%fused_computation.21 | convolution fusion | flops 12582912 | bytes 4227072 | tf_op jit(solution)/shard_map/tij,ti->tj/dot_general | solution.py:60
  17.4 6.0 %all-to-all-start.1 = ((f32[8,2,256]{2,1,0:T(2,128)}), f32[8,2,256]{2,1,0:T(2,128)S(1)}, u32[]{:S(2)}, u32[]{:S(2)}) async-start(f32[8,2,256]{2,1,0:T(2,128)} %all_to_all.63), calls=%async_computation.1 | async-start | bytes 32768 | tf_op jit(solution)/shard_map/all_to_all | solution.py:93
  23.4 5.7 %fusion.12 = f32[16,1,256]{2,1,0:T(1,128)S(1)} fusion(f32[1,1,16,256,256]{4,3,2,1,0:T(8,128)} %param.12, f32[16,256,1]{1,0,2:T(8,128)S(1)} %bitcast.154), kind=kOutput, calls=%fused_computation.17 | convolution fusion | flops 12582912 | bytes 4227072 | tf_op jit(solution)/shard_map/tij,tj->ti/dot_general | solution.py:54
  33.8 6.0 %all-to-all-start.2 = ((f32[8,2,256]{2,1,0:T(2,128)}), f32[8,2,256]{2,1,0:T(2,128)S(1)}, u32[]{:S(2)}, u32[]{:S(2)}) async-start(f32[8,2,256]{2,1,0:T(2,128)} %copy.28), calls=%async_computation.2 | async-start | bytes 32768 | tf_op jit(solution)/shard_map/all_to_all | solution.py:111
  40.0 6.5 %all-to-all-done.2 = f32[8,2,256]{2,1,0:T(2,128)S(1)} async-done(((f32[8,2,256]{2,1,0:T(2,128)}), f32[8,2,256]{2,1,0:T(2,128)S(1)}, u32[]{:S(2)}, u32[]{:S(2)}) %all-to-all-start.2) | async-done | bytes 16416 | tf_op jit(solution)/shard_map/all_to_all | solution.py:111
  46.6 5.7 %fusion.14 = f32[16,1,256]{2,1,0:T(1,128)S(1)} fusion(f32[1,1,16,256,256]{4,3,2,1,0:T(8,128)} %param.12, f32[16,256,1]{1,0,2:T(8,128)S(1)} %convolution_bitcast_fusion.6), kind=kOutput, calls=%fused_computation.19 | convolution fusion | flops 12582912 | bytes 4227072 | tf_op jit(solution)/shard_map/tij,tj->ti/dot_general | solution.py:54
  52.4 10.5 %all-reduce.3 = (f32[16,256]{1,0:T(8,128)S(1)}, f32[16,256]{1,0:T(8,128)S(1)}) all-reduce(f32[16,256]{1,0:T(8,128)S(1)} %fusion.30, f32[16,256]{1,0:T(8,128)S(1)} %fusion.32), channel_id=1, replica_groups=mesh['row'=8,'col'=4] {'col'}, use_global_device_ids=true, to_apply=%region_7.8 | all-reduce | flops 8192 | bytes 65536 | tf_op jit(solution)/shard_map/psum | solution.py:56
  64.2 4.3 %fusion.10 = f32[16,1,256]{2,1,0:T(1,128)S(1)} fusion(f32[1,1,16,256,256]{4,3,2,1,0:T(8,128)} %param.12, f32[16,256,1]{1,0,2:T(8,128)S(1)} %bitcast.157), kind=kOutput, calls=%fused_computation.15 | convolution fusion | flops 12582912 | bytes 4227072 | tf_op jit(solution)/shard_map/tij,ti->tj/dot_general | solution.py:60
  72.6 22.5 %all-reduce.2 = (f32[]{:T(128)}, f32[]{:T(128)}, f32[]{:T(128)}) all-reduce(f32[]{:T(128)} %get-tuple-element.29, f32[]{:T(128)} %get-tuple-element.7, f32[]{:T(128)} %get-tuple-element.6), channel_id=1, replica_groups=mesh['row'=8,'col'=4] {'row'}, use_global_device_ids=true, to_apply=%region_4.5 | all-reduce | flops 3 | bytes 24 | tf_op jit(solution)/shard_map/psum | solution.py:123
  95.1 6.3 %psum.120 = f32[]{:T(128)} all-reduce(f32[]{:T(128)} %get-tuple-element.16), channel_id=1, replica_groups=mesh['row'=8,'col'=4] {'col'}, use_global_device_ids=true, to_apply=%region_5.6 | all-reduce | flops 1 | bytes 8 | tf_op jit(solution)/shard_map/psum | solution.py:124
  108.4 6.5 %all-to-all-done.4 = f32[8,2,256]{2,1,0:T(2,128)S(1)} async-done(((f32[8,2,256]{2,1,0:T(2,128)}), f32[8,2,256]{2,1,0:T(2,128)S(1)}, u32[]{:S(2)}, u32[]{:S(2)}) %all-to-all-start.4) | async-done | bytes 16416 | tf_op jit(solution)/shard_map/all_to_all | solution.py:111
  115.1 5.7 %fusion.8 = f32[16,1,256]{2,1,0:T(1,128)S(1)} fusion(f32[1,1,16,256,256]{4,3,2,1,0:T(8,128)} %param.12, f32[16,256,1]{1,0,2:T(8,128)S(1)} %convolution_bitcast_fusion.4), kind=kOutput, calls=%fused_computation.13 | convolution fusion | flops 12582912 | bytes 4227072 | tf_op jit(solution)/shard_map/tij,tj->ti/dot_general | solution.py:54
  120.9 10.1 %psum.127 = f32[16,256]{1,0:T(8,128)S(1)} all-reduce(f32[16,256]{1,0:T(8,128)S(1)} %fusion.26), channel_id=1, replica_groups=mesh['row'=8,'col'=4] {'col'}, use_global_device_ids=true, to_apply=%region_15.16 | all-reduce | flops 4096 | bytes 32768 | tf_op jit(solution)/shard_map/psum | solution.py:56
  140.7 22.5 %all-reduce.1 = (f32[]{:T(128)}, f32[]{:T(128)}, f32[]{:T(128)}) all-reduce(f32[]{:T(128)} %get-tuple-element.25, f32[]{:T(128)} %get-tuple-element.5, f32[]{:T(128)} %get-tuple-element.4), channel_id=1, replica_groups=mesh['row'=8,'col'=4] {'row'}, use_global_device_ids=true, to_apply=%region_13.14 | all-reduce | flops 3 | bytes 24 | tf_op jit(solution)/shard_map/psum | solution.py:123
  163.1 6.3 %psum.126 = f32[]{:T(128)} all-reduce(f32[]{:T(128)} %get-tuple-element.13), channel_id=1, replica_groups=mesh['row'=8,'col'=4] {'col'}, use_global_device_ids=true, to_apply=%region_14.15 | all-reduce | flops 1 | bytes 8 | tf_op jit(solution)/shard_map/psum | solution.py:124
  176.7 6.3 %all-to-all-done.6 = f32[8,2,256]{2,1,0:T(2,128)S(1)} async-done(((f32[8,2,256]{2,1,0:T(2,128)}), f32[8,2,256]{2,1,0:T(2,128)S(1)}, u32[]{:S(2)}, u32[]{:S(2)}) %all-to-all-start.6) | async-done | bytes 16416 | tf_op jit(solution)/shard_map/all_to_all | solution.py:111
  183.1 5.7 %fusion.4 = f32[16,1,256]{2,1,0:T(1,128)S(1)} fusion(f32[1,1,16,256,256]{4,3,2,1,0:T(8,128)} %param.12, f32[16,256,1]{1,0,2:T(8,128)S(1)} %convolution_bitcast_fusion.2), kind=kOutput, calls=%fused_computation.9 | convolution fusion | flops 12582912 | bytes 4227072 | tf_op jit(solution)/shard_map/tij,tj->ti/dot_general | solution.py:54
  188.9 10.1 %psum.132 = f32[16,256]{1,0:T(8,128)S(1)} all-reduce(f32[16,256]{1,0:T(8,128)S(1)} %fusion.22), channel_id=1, replica_groups=mesh['row'=8,'col'=4] {'col'}, use_global_device_ids=true, to_apply=%region_23.24 | all-reduce | flops 4096 | bytes 32768 | tf_op jit(solution)/shard_map/psum | solution.py:56
  208.7 22.5 %all-reduce = (f32[]{:T(128)}, f32[]{:T(128)}, f32[]{:T(128)}) all-reduce(f32[]{:T(128)} %get-tuple-element.22, f32[]{:T(128)} %get-tuple-element.3, f32[]{:T(128)} %get-tuple-element.2), channel_id=1, replica_groups=mesh['row'=8,'col'=4] {'row'}, use_global_device_ids=true, to_apply=%region_21.22 | all-reduce | flops 3 | bytes 24 | tf_op jit(solution)/shard_map/psum | solution.py:123
  231.2 6.3 %psum.131 = f32[]{:T(128)} all-reduce(f32[]{:T(128)} %get-tuple-element.10), channel_id=1, replica_groups=mesh['row'=8,'col'=4] {'col'}, use_global_device_ids=true, to_apply=%region_22.23 | all-reduce | flops 1 | bytes 8 | tf_op jit(solution)/shard_map/psum | solution.py:124
  243.9 31.0 %all_gather.3 = f32[32768]{0:T(1024)S(1)} all-gather(f32[4096]{0:T(1024)S(1)} %minimum_select_fusion), channel_id=1, replica_groups=mesh['row'=8,'col'=4] {'row'}, dimensions={0}, use_global_device_ids=true | all-gather | bytes 147456 | tf_op jit(solution)/shard_map/all_gather | solution.py:129
  275.8 5.7 %fusion = f32[16,1,256]{2,1,0:T(1,128)S(1)} fusion(f32[1,1,16,256,256]{4,3,2,1,0:T(8,128)} %param.12, f32[16,256,1]{1,0,2:T(8,128)S(1)} %convolution_bitcast_fusion), kind=kOutput, calls=%fused_computation.5 | convolution fusion | flops 12582912 | bytes 4227072 | tf_op jit(solution)/shard_map/tij,tj->ti/dot_general | solution.py:54
  281.6 10.1 %psum.135 = f32[16,256]{1,0:T(8,128)S(1)} all-reduce(f32[16,256]{1,0:T(8,128)S(1)} %fusion.18), channel_id=1, replica_groups=mesh['row'=8,'col'=4] {'col'}, use_global_device_ids=true, to_apply=%region_28.29 | all-reduce | flops 4096 | bytes 32768 | tf_op jit(solution)/shard_map/psum | solution.py:56
  (108 shorter events, 50.2 us)
Async XLA Ops:
  0.6 16.2 %copy-start.1 = (f32[128,256]{1,0:T(8,128)S(1)}, f32[128,256]{1,0:T(8,128)}, u32[]{:S(2)}) copy-start(f32[128,256]{1,0:T(8,128)} %param.20) | copy-start | bytes 393220
  2.4 15.0 %all-to-all-start = ((s32[8,2,1]{1,2,0:T(1,128)}), s32[8,2,1]{1,2,0:T(1,128)S(1)}, u32[]{:S(2)}, u32[]{:S(2)}) async-start(s32[8,2,1]{1,2,0:T(1,128)} %bitcast.1), calls=%async_computation | async-start | bytes 8192 | tf_op jit(solution)/shard_map/all_to_all | solution.py:82
  11.6 18.8 %copy-start.3 = (f32[128,256]{1,0:T(8,128)S(1)}, f32[128,256]{1,0:T(8,128)}, u32[]{:S(2)}) copy-start(f32[128,256]{1,0:T(8,128)} %param.14) | copy-start | bytes 393220
  11.7 18.9 %copy-start.4 = (f32[128,256]{1,0:T(8,128)S(1)}, f32[128,256]{1,0:T(8,128)}, u32[]{:S(2)}) copy-start(f32[128,256]{1,0:T(8,128)} %param.15) | copy-start | bytes 393220
  11.7 18.9 %copy-start.5 = (f32[128,256]{1,0:T(8,128)S(1)}, f32[128,256]{1,0:T(8,128)}, u32[]{:S(2)}) copy-start(f32[128,256]{1,0:T(8,128)} %param.16) | copy-start | bytes 393220
  11.7 19.0 %copy-start.6 = (s32[128,256]{1,0:T(8,128)S(1)}, s32[128,256]{1,0:T(8,128)}, u32[]{:S(2)}) copy-start(s32[128,256]{1,0:T(8,128)} %param.17) | copy-start | bytes 393220
  17.4 14.8 %all-to-all-start.1 = ((f32[8,2,256]{2,1,0:T(2,128)}), f32[8,2,256]{2,1,0:T(2,128)S(1)}, u32[]{:S(2)}, u32[]{:S(2)}) async-start(f32[8,2,256]{2,1,0:T(2,128)} %all_to_all.63), calls=%async_computation.1 | async-start | bytes 32768 | tf_op jit(solution)/shard_map/all_to_all | solution.py:93
  23.4 39.5 %copy-start = (f32[16,256]{1,0:T(8,128)S(1)}, f32[16,256]{1,0:T(8,128)}, u32[]{:S(2)}) copy-start(f32[16,256]{1,0:T(8,128)} %param.21) | copy-start | bytes 49156
  23.4 39.5 %copy-start.2 = (f32[16,256]{1,0:T(8,128)S(1)}, f32[16,256]{1,0:T(8,128)}, u32[]{:S(2)}) copy-start(f32[16,256]{1,0:T(8,128)} %param.18) | copy-start | bytes 49156
  23.4 39.5 %copy-start.7 = (s32[16,256]{1,0:T(8,128)S(1)}, s32[16,256]{1,0:T(8,128)}, u32[]{:S(2)}) copy-start(s32[16,256]{1,0:T(8,128)} %param.19) | copy-start | bytes 49156
  33.8 12.6 %all-to-all-start.2 = ((f32[8,2,256]{2,1,0:T(2,128)}), f32[8,2,256]{2,1,0:T(2,128)S(1)}, u32[]{:S(2)}, u32[]{:S(2)}) async-start(f32[8,2,256]{2,1,0:T(2,128)} %copy.28), calls=%async_computation.2 | async-start | bytes 32768 | tf_op jit(solution)/shard_map/all_to_all | solution.py:111
  69.3 34.1 %all-to-all-start.3 = ((f32[8,2,256]{2,1,0:T(2,128)}), f32[8,2,256]{2,1,0:T(2,128)S(1)}, u32[]{:S(2)}, u32[]{:S(2)}) async-start(f32[8,2,256]{2,1,0:T(2,128)} %all_to_all.69), calls=%async_computation.3 | async-start | bytes 32768 | tf_op jit(solution)/shard_map/all_to_all | solution.py:93
  105.0 9.9 %all-to-all-start.4 = ((f32[8,2,256]{2,1,0:T(2,128)}), f32[8,2,256]{2,1,0:T(2,128)S(1)}, u32[]{:S(2)}, u32[]{:S(2)}) async-start(f32[8,2,256]{2,1,0:T(2,128)} %copy.29), calls=%async_computation.4 | async-start | bytes 32768 | tf_op jit(solution)/shard_map/all_to_all | solution.py:111
  137.3 34.1 %all-to-all-start.5 = ((f32[8,2,256]{2,1,0:T(2,128)}), f32[8,2,256]{2,1,0:T(2,128)S(1)}, u32[]{:S(2)}, u32[]{:S(2)}) async-start(f32[8,2,256]{2,1,0:T(2,128)} %all_to_all.74), calls=%async_computation.5 | async-start | bytes 32768 | tf_op jit(solution)/shard_map/all_to_all | solution.py:93
  173.1 9.9 %all-to-all-start.6 = ((f32[8,2,256]{2,1,0:T(2,128)}), f32[8,2,256]{2,1,0:T(2,128)S(1)}, u32[]{:S(2)}, u32[]{:S(2)}) async-start(f32[8,2,256]{2,1,0:T(2,128)} %copy.30), calls=%async_computation.6 | async-start | bytes 32768 | tf_op jit(solution)/shard_map/all_to_all | solution.py:111
  205.4 34.2 %all-to-all-start.7 = ((f32[8,2,256]{2,1,0:T(2,128)}), f32[8,2,256]{2,1,0:T(2,128)S(1)}, u32[]{:S(2)}, u32[]{:S(2)}) async-start(f32[8,2,256]{2,1,0:T(2,128)} %all_to_all.79), calls=%async_computation.7 | async-start | bytes 32768 | tf_op jit(solution)/shard_map/all_to_all | solution.py:93
  240.6 35.0 %all-to-all-start.8 = ((f32[8,2,256]{2,1,0:T(2,128)}), f32[8,2,256]{2,1,0:T(2,128)S(1)}, u32[]{:S(2)}, u32[]{:S(2)}) async-start(f32[8,2,256]{2,1,0:T(2,128)} %copy.31), calls=%async_computation.8 | async-start | bytes 32768 | tf_op jit(solution)/shard_map/all_to_all | solution.py:111
where the time goes:
time: 294 us; the launch traced here: 292 us
  blocking collectives  158 us (54%)
  matrix products  48.7 us (17%)
  starting transfers between devices  39.6 us (13%)
  waiting for transfers between devices  19.2 us (7%)
  local copies, waits for them, and re-layouts  11.3 us (4%)
  between operations  8.64 us (3%)
  other arithmetic  6.96 us (2%)
    psum x3, blocking collectives, shards(): lax.psum((cross_part, dual_part, primal_part), 'row')  67.4 us
    psum x4, blocking collectives, forward_picked(): return lax.psum(partial_rows, 'col')  40.9 us
    all_gather x1, blocking collectives, shards(): lax.all_gather(primal, 'row', axis=0, tiled=True)  31 us
    dot_general x5, matrix products, forward_picked(): product = jnp.einsum('tij,tj->ti', tile_set, picked, precision=highest)  28.3 us
    all_to_all x4, waiting for transfers between devices, shards(): lax.all_to_all(back, 'row', split_axis=0, concat_axis=0, tiled=True)  19.2 us
    psum x3, blocking collectives, shards(): primal_square = lax.psum(primal_rows, 'col')  18.8 us
    dot_general x4, matrix products, backward_product(): return jnp.einsum('tij,ti->tj', tile_set, picked, precision=highest)  17.2 us
    all_to_all x4, starting transfers between devices, shards(): lax.all_to_all(back, 'row', split_axis=0, concat_axis=0, tiled=True)  16.2 us
  transfers between devices with their start and end apart: 9, of which 3 were waited for; matrix products, arithmetic and copies ran while one was open for 5% of the time, Pallas kernels for 0%

commit v1 on v0

--- a/solution.py
+++ b/solution.py
@@ -53,7 +53,7 @@
     def forward_picked(picked):
         product = jnp.einsum("tij,tj->ti", tile_set, picked, precision=highest)
         partial_rows = jnp.dot(row_onehot, product, precision=highest)
-        return lax.psum(partial_rows, "col")
+        return jnp.sum(lax.all_gather(partial_rows, "col"), axis=0)
 
     def backward_product(vector):
         picked = vector[row_of]

time: 294 us -> 276 us (0.939)
  blocking collectives: 158 us -> 144 us
  waiting for transfers between devices: 19.2 us -> 13.9 us
    psum x4 -> x0, blocking collectives: 40.9 us -> none  [forward_picked(): return lax.psum(partial_rows, 'col')]
    all_gather x0 -> x5, blocking collectives: none -> 26.4 us  [forward_picked(): return jnp.sum(lax.all_gather(partial_rows, 'col'), axis=0)]
    all_to_all x4, waiting for transfers between devices: 19.2 us -> 13.9 us  [shards(): lax.all_to_all(back, 'row', split_axis=0, concat_axis=0, tiled=True)]
  transfers between devices with their start and end apart: 9 -> 9, of which waited for: 3 -> 3; matrix products, arithmetic and copies ran while one was open for 5% -> 6% of each run, Pallas kernels for 0% -> 0%
where the time goes in v1:
time: 276 us; the launch traced here: 274 us
  blocking collectives  144 us (52%)
  matrix products  48.7 us (18%)
  starting transfers between devices  41 us (15%)
  waiting for transfers between devices  13.9 us (5%)
  local copies, waits for them, and re-layouts  11.3 us (4%)
  between operations  8.62 us (3%)
  other arithmetic  6.99 us (3%)
    psum x3, blocking collectives, shards(): lax.psum((cross_part, dual_part, primal_part), 'row')  67.5 us
    all_gather x1, blocking collectives, shards(): lax.all_gather(primal, 'row', axis=0, tiled=True)  31 us
    dot_general x5, matrix products, forward_picked(): product = jnp.einsum('tij,tj->ti', tile_set, picked, precision=highest)  28.3 us
    all_gather x5, blocking collectives, forward_picked(): return jnp.sum(lax.all_gather(partial_rows, 'col'), axis=0)  26.4 us
    psum x3, blocking collectives, shards(): primal_square = lax.psum(primal_rows, 'col')  18.8 us
    all_to_all x4, starting transfers between devices, reduce_back(): lax.all_to_all(sent, 'row', split_axis=0, concat_axis=0, tiled=True)  17.5 us
    dot_general x4, matrix products, backward_product(): return jnp.einsum('tij,ti->tj', tile_set, picked, precision=highest)  17.2 us
    all_to_all x4, starting transfers between devices, shards(): lax.all_to_all(back, 'row', split_axis=0, concat_axis=0, tiled=True)  16.2 us
  transfers between devices with their start and end apart: 9, of which 3 were waited for; matrix products, arithmetic and copies ran while one was open for 6% of the time, Pallas kernels for 0%

profile of v1, /device:TPU:0, one launch (start us, length us, event | category | flops | bytes accessed | tf_op | source)
XLA Modules:
  0.0 274.2 jit_solution(14328628505180261410)
XLA Ops:
  2.4 7.3 %all-to-all-start = ((s32[8,2,1]{1,2,0:T(1,128)}), s32[8,2,1]{1,2,0:T(1,128)S(1)}, u32[]{:S(2)}, u32[]{:S(2)}) async-start(s32[8,2,1]{1,2,0:T(1,128)} %bitcast.1), calls=%async_computation | async-start | bytes 8192 | tf_op jit(solution)/shard_map/all_to_all | solution.py:82
  11.7 4.3 %fusion.16 = f32[16,1,256]{2,1,0:T(1,128)S(1)} fusion(f32[1,1,16,256,256]{4,3,2,1,0:T(8,128)} %param.12, f32[16,256,1]{1,0,2:T(8,128)S(1)} %bitcast.166), kind=kOutput, calls=%fused_computation.21 | convolution fusion | flops 12582912 | bytes 4227072 | tf_op jit(solution)/shard_map/tij,ti->tj/dot_general | solution.py:60
  17.4 6.0 %all-to-all-start.1 = ((f32[8,2,256]{2,1,0:T(2,128)}), f32[8,2,256]{2,1,0:T(2,128)S(1)}, u32[]{:S(2)}, u32[]{:S(2)}) async-start(f32[8,2,256]{2,1,0:T(2,128)} %all_to_all.63), calls=%async_computation.1 | async-start | bytes 32768 | tf_op jit(solution)/shard_map/all_to_all | solution.py:93
  23.4 5.7 %fusion.12 = f32[16,1,256]{2,1,0:T(1,128)S(1)} fusion(f32[1,1,16,256,256]{4,3,2,1,0:T(8,128)} %param.12, f32[16,256,1]{1,0,2:T(8,128)S(1)} %bitcast.164), kind=kOutput, calls=%fused_computation.17 | convolution fusion | flops 12582912 | bytes 4227072 | tf_op jit(solution)/shard_map/tij,tj->ti/dot_general | solution.py:54
  33.8 6.0 %all-to-all-start.2 = ((f32[8,2,256]{2,1,0:T(2,128)}), f32[8,2,256]{2,1,0:T(2,128)S(1)}, u32[]{:S(2)}, u32[]{:S(2)}) async-start(f32[8,2,256]{2,1,0:T(2,128)} %copy.28), calls=%async_computation.2 | async-start | bytes 32768 | tf_op jit(solution)/shard_map/all_to_all | solution.py:111
  40.0 5.2 %all-gather.1 = f32[64,256]{1,0:T(8,128)S(1)} all-gather(f32[16,256]{1,0:T(8,128)S(1)} %fusion.30), channel_id=3, replica_groups=mesh['row'=8,'col'=4] {'col'}, dimensions={0}, use_global_device_ids=true | all-gather | bytes 81920 | tf_op jit(solution)/shard_map/all_gather | solution.py:56
  46.6 5.7 %fusion.14 = f32[16,1,256]{2,1,0:T(1,128)S(1)} fusion(f32[1,1,16,256,256]{4,3,2,1,0:T(8,128)} %param.12, f32[16,256,1]{1,0,2:T(8,128)S(1)} %convolution_bitcast_fusion.6), kind=kOutput, calls=%fused_computation.19 | convolution fusion | flops 12582912 | bytes 4227072 | tf_op jit(solution)/shard_map/tij,tj->ti/dot_general | solution.py:54
  52.4 5.4 %all-gather = f32[64,256]{1,0:T(8,128)S(1)} all-gather(f32[16,256]{1,0:T(8,128)S(1)} %fusion.32), channel_id=2, replica_groups=mesh['row'=8,'col'=4] {'col'}, dimensions={0}, use_global_device_ids=true | all-gather | bytes 81920 | tf_op jit(solution)/shard_map/all_gather | solution.py:56
  64.2 4.8 %all-to-all-start.3 = ((f32[8,2,256]{2,1,0:T(2,128)}), f32[8,2,256]{2,1,0:T(2,128)S(1)}, u32[]{:S(2)}, u32[]{:S(2)}) async-start(f32[8,2,256]{2,1,0:T(2,128)} %all_to_all.69), calls=%async_computation.3 | async-start | bytes 32768 | tf_op jit(solution)/shard_map/all_to_all | solution.py:93
  69.0 22.5 %all-reduce.2 = (f32[]{:T(128)}, f32[]{:T(128)}, f32[]{:T(128)}) all-reduce(f32[]{:T(128)} %get-tuple-element.27, f32[]{:T(128)} %get-tuple-element.7, f32[]{:T(128)} %get-tuple-element.6), channel_id=1, replica_groups=mesh['row'=8,'col'=4] {'row'}, use_global_device_ids=true, to_apply=%region_4.5 | all-reduce | flops 3 | bytes 24 | tf_op jit(solution)/shard_map/psum | solution.py:123
  91.5 6.3 %psum.85 = f32[]{:T(128)} all-reduce(f32[]{:T(128)} %get-tuple-element.16), channel_id=1, replica_groups=mesh['row'=8,'col'=4] {'col'}, use_global_device_ids=true, to_apply=%region_5.6 | all-reduce | flops 1 | bytes 8 | tf_op jit(solution)/shard_map/psum | solution.py:124
  104.8 6.5 %all-to-all-done.4 = f32[8,2,256]{2,1,0:T(2,128)S(1)} async-done(((f32[8,2,256]{2,1,0:T(2,128)}), f32[8,2,256]{2,1,0:T(2,128)S(1)}, u32[]{:S(2)}, u32[]{:S(2)}) %all-to-all-start.4) | async-done | bytes 16416 | tf_op jit(solution)/shard_map/all_to_all | solution.py:111
  111.5 5.7 %fusion.8 = f32[16,1,256]{2,1,0:T(1,128)S(1)} fusion(f32[1,1,16,256,256]{4,3,2,1,0:T(8,128)} %param.12, f32[16,256,1]{1,0,2:T(8,128)S(1)} %convolution_bitcast_fusion.4), kind=kOutput, calls=%fused_computation.13 | convolution fusion | flops 12582912 | bytes 4227072 | tf_op jit(solution)/shard_map/tij,tj->ti/dot_general | solution.py:54
  117.3 5.2 %all-gather.2 = f32[64,256]{1,0:T(8,128)S(1)} all-gather(f32[16,256]{1,0:T(8,128)S(1)} %fusion.26), channel_id=4, replica_groups=mesh['row'=8,'col'=4] {'col'}, dimensions={0}, use_global_device_ids=true | all-gather | bytes 81920 | tf_op jit(solution)/shard_map/all_gather | solution.py:56
  132.2 22.5 %all-reduce.1 = (f32[]{:T(128)}, f32[]{:T(128)}, f32[]{:T(128)}) all-reduce(f32[]{:T(128)} %get-tuple-element.23, f32[]{:T(128)} %get-tuple-element.5, f32[]{:T(128)} %get-tuple-element.4), channel_id=1, replica_groups=mesh['row'=8,'col'=4] {'row'}, use_global_device_ids=true, to_apply=%region_13.14 | all-reduce | flops 3 | bytes 24 | tf_op jit(solution)/shard_map/psum | solution.py:123
  154.7 6.3 %psum.89 = f32[]{:T(128)} all-reduce(f32[]{:T(128)} %get-tuple-element.13), channel_id=1, replica_groups=mesh['row'=8,'col'=4] {'col'}, use_global_device_ids=true, to_apply=%region_14.15 | all-reduce | flops 1 | bytes 8 | tf_op jit(solution)/shard_map/psum | solution.py:124
  168.2 6.3 %all-to-all-done.6 = f32[8,2,256]{2,1,0:T(2,128)S(1)} async-done(((f32[8,2,256]{2,1,0:T(2,128)}), f32[8,2,256]{2,1,0:T(2,128)S(1)}, u32[]{:S(2)}, u32[]{:S(2)}) %all-to-all-start.6) | async-done | bytes 16416 | tf_op jit(solution)/shard_map/all_to_all | solution.py:111
  174.7 5.7 %fusion.4 = f32[16,1,256]{2,1,0:T(1,128)S(1)} fusion(f32[1,1,16,256,256]{4,3,2,1,0:T(8,128)} %param.12, f32[16,256,1]{1,0,2:T(8,128)S(1)} %convolution_bitcast_fusion.2), kind=kOutput, calls=%fused_computation.9 | convolution fusion | flops 12582912 | bytes 4227072 | tf_op jit(solution)/shard_map/tij,tj->ti/dot_general | solution.py:54
  180.5 5.2 %all-gather.3 = f32[64,256]{1,0:T(8,128)S(1)} all-gather(f32[16,256]{1,0:T(8,128)S(1)} %fusion.22), channel_id=5, replica_groups=mesh['row'=8,'col'=4] {'col'}, dimensions={0}, use_global_device_ids=true | all-gather | bytes 81920 | tf_op jit(solution)/shard_map/all_gather | solution.py:56
  195.4 22.5 %all-reduce = (f32[]{:T(128)}, f32[]{:T(128)}, f32[]{:T(128)}) all-reduce(f32[]{:T(128)} %get-tuple-element.20, f32[]{:T(128)} %get-tuple-element.3, f32[]{:T(128)} %get-tuple-element.2), channel_id=1, replica_groups=mesh['row'=8,'col'=4] {'row'}, use_global_device_ids=true, to_apply=%region_21.22 | all-reduce | flops 3 | bytes 24 | tf_op jit(solution)/shard_map/psum | solution.py:123
  217.9 6.3 %psum.93 = f32[]{:T(128)} all-reduce(f32[]{:T(128)} %get-tuple-element.10), channel_id=1, replica_groups=mesh['row'=8,'col'=4] {'col'}, use_global_device_ids=true, to_apply=%region_22.23 | all-reduce | flops 1 | bytes 8 | tf_op jit(solution)/shard_map/psum | solution.py:124
  230.6 31.0 %all_gather.41 = f32[32768]{0:T(1024)S(1)} all-gather(f32[4096]{0:T(1024)S(1)} %minimum_select_fusion), channel_id=1, replica_groups=mesh['row'=8,'col'=4] {'row'}, dimensions={0}, use_global_device_ids=true | all-gather | bytes 147456 | tf_op jit(solution)/shard_map/all_gather | solution.py:129
  262.5 5.7 %fusion = f32[16,1,256]{2,1,0:T(1,128)S(1)} fusion(f32[1,1,16,256,256]{4,3,2,1,0:T(8,128)} %param.12, f32[16,256,1]{1,0,2:T(8,128)S(1)} %convolution_bitcast_fusion), kind=kOutput, calls=%fused_computation.5 | convolution fusion | flops 12582912 | bytes 4227072 | tf_op jit(solution)/shard_map/tij,tj->ti/dot_general | solution.py:54
  268.3 5.2 %all-gather.4 = f32[64,256]{1,0:T(8,128)S(1)} all-gather(f32[16,256]{1,0:T(8,128)S(1)} %fusion.18), channel_id=6, replica_groups=mesh['row'=8,'col'=4] {'col'}, dimensions={0}, use_global_device_ids=true | all-gather | bytes 81920 | tf_op jit(solution)/shard_map/all_gather | solution.py:56
  (114 shorter events, 52.4 us)
Async XLA Ops:
  0.6 16.2 %copy-start.1 = (f32[128,256]{1,0:T(8,128)S(1)}, f32[128,256]{1,0:T(8,128)}, u32[]{:S(2)}) copy-start(f32[128,256]{1,0:T(8,128)} %param.20) | copy-start | bytes 393220
  2.4 15.0 %all-to-all-start = ((s32[8,2,1]{1,2,0:T(1,128)}), s32[8,2,1]{1,2,0:T(1,128)S(1)}, u32[]{:S(2)}, u32[]{:S(2)}) async-start(s32[8,2,1]{1,2,0:T(1,128)} %bitcast.1), calls=%async_computation | async-start | bytes 8192 | tf_op jit(solution)/shard_map/all_to_all | solution.py:82
  11.6 18.8 %copy-start.3 = (f32[128,256]{1,0:T(8,128)S(1)}, f32[128,256]{1,0:T(8,128)}, u32[]{:S(2)}) copy-start(f32[128,256]{1,0:T(8,128)} %param.14) | copy-start | bytes 393220
  11.7 18.8 %copy-start.4 = (f32[128,256]{1,0:T(8,128)S(1)}, f32[128,256]{1,0:T(8,128)}, u32[]{:S(2)}) copy-start(f32[128,256]{1,0:T(8,128)} %param.15) | copy-start | bytes 393220
  11.7 18.9 %copy-start.5 = (f32[128,256]{1,0:T(8,128)S(1)}, f32[128,256]{1,0:T(8,128)}, u32[]{:S(2)}) copy-start(f32[128,256]{1,0:T(8,128)} %param.16) | copy-start | bytes 393220
  11.7 19.0 %copy-start.6 = (s32[128,256]{1,0:T(8,128)S(1)}, s32[128,256]{1,0:T(8,128)}, u32[]{:S(2)}) copy-start(s32[128,256]{1,0:T(8,128)} %param.17) | copy-start | bytes 393220
  17.4 14.8 %all-to-all-start.1 = ((f32[8,2,256]{2,1,0:T(2,128)}), f32[8,2,256]{2,1,0:T(2,128)S(1)}, u32[]{:S(2)}, u32[]{:S(2)}) async-start(f32[8,2,256]{2,1,0:T(2,128)} %all_to_all.63), calls=%async_computation.1 | async-start | bytes 32768 | tf_op jit(solution)/shard_map/all_to_all | solution.py:93
  29.1 28.8 %copy-start = (f32[16,256]{1,0:T(8,128)S(1)}, f32[16,256]{1,0:T(8,128)}, u32[]{:S(2)}) copy-start(f32[16,256]{1,0:T(8,128)} %param.21) | copy-start | bytes 49156
  29.1 28.8 %copy-start.2 = (f32[16,256]{1,0:T(8,128)S(1)}, f32[16,256]{1,0:T(8,128)}, u32[]{:S(2)}) copy-start(f32[16,256]{1,0:T(8,128)} %param.18) | copy-start | bytes 49156
  29.1 28.8 %copy-start.7 = (s32[16,256]{1,0:T(8,128)S(1)}, s32[16,256]{1,0:T(8,128)}, u32[]{:S(2)}) copy-start(s32[16,256]{1,0:T(8,128)} %param.19) | copy-start | bytes 49156
  33.8 12.6 %all-to-all-start.2 = ((f32[8,2,256]{2,1,0:T(2,128)}), f32[8,2,256]{2,1,0:T(2,128)S(1)}, u32[]{:S(2)}, u32[]{:S(2)}) async-start(f32[8,2,256]{2,1,0:T(2,128)} %copy.28), calls=%async_computation.2 | async-start | bytes 32768 | tf_op jit(solution)/shard_map/all_to_all | solution.py:111
  64.2 35.6 %all-to-all-start.3 = ((f32[8,2,256]{2,1,0:T(2,128)}), f32[8,2,256]{2,1,0:T(2,128)S(1)}, u32[]{:S(2)}, u32[]{:S(2)}) async-start(f32[8,2,256]{2,1,0:T(2,128)} %all_to_all.69), calls=%async_computation.3 | async-start | bytes 32768 | tf_op jit(solution)/shard_map/all_to_all | solution.py:93
  101.5 9.9 %all-to-all-start.4 = ((f32[8,2,256]{2,1,0:T(2,128)}), f32[8,2,256]{2,1,0:T(2,128)S(1)}, u32[]{:S(2)}, u32[]{:S(2)}) async-start(f32[8,2,256]{2,1,0:T(2,128)} %copy.29), calls=%async_computation.4 | async-start | bytes 32768 | tf_op jit(solution)/shard_map/all_to_all | solution.py:111
  128.9 34.1 %all-to-all-start.5 = ((f32[8,2,256]{2,1,0:T(2,128)}), f32[8,2,256]{2,1,0:T(2,128)S(1)}, u32[]{:S(2)}, u32[]{:S(2)}) async-start(f32[8,2,256]{2,1,0:T(2,128)} %all_to_all.74), calls=%async_computation.5 | async-start | bytes 32768 | tf_op jit(solution)/shard_map/all_to_all | solution.py:93
  164.6 9.9 %all-to-all-start.6 = ((f32[8,2,256]{2,1,0:T(2,128)}), f32[8,2,256]{2,1,0:T(2,128)S(1)}, u32[]{:S(2)}, u32[]{:S(2)}) async-start(f32[8,2,256]{2,1,0:T(2,128)} %copy.30), calls=%async_computation.6 | async-start | bytes 32768 | tf_op jit(solution)/shard_map/all_to_all | solution.py:111
  192.0 34.2 %all-to-all-start.7 = ((f32[8,2,256]{2,1,0:T(2,128)}), f32[8,2,256]{2,1,0:T(2,128)S(1)}, u32[]{:S(2)}, u32[]{:S(2)}) async-start(f32[8,2,256]{2,1,0:T(2,128)} %all_to_all.79), calls=%async_computation.7 | async-start | bytes 32768 | tf_op jit(solution)/shard_map/all_to_all | solution.py:93
  227.3 35.0 %all-to-all-start.8 = ((f32[8,2,256]{2,1,0:T(2,128)}), f32[8,2,256]{2,1,0:T(2,128)S(1)}, u32[]{:S(2)}, u32[]{:S(2)}) async-start(f32[8,2,256]{2,1,0:T(2,128)} %copy.31), calls=%async_computation.8 | async-start | bytes 32768 | tf_op jit(solution)/shard_map/all_to_all | solution.py:111
